TPU v7x, 128 devices: a whole 4x4x4 slice. The times are simulated.
128 devices in a mesh: patch: 64 (over y, x_hi, z, core), band: 2 (over x_lo).
Axes of the slice: x: 4 (x_hi: 2, x_lo: 2; x = x_hi * 2 + x_lo), y: 4, z: 4, core: 2. Of those that a mesh axis runs over, the one named last changes fastest.
Arguments:
- latents: float32 [40960, 512], P('patch', 'band'), may hold values from -6 to 6
- edge_latents: float32 [327680, 512], P(('patch', 'band')), may hold values from -6 to 6
- edge_sender: int32 [327680], P(('patch', 'band')), may hold values from 0 to 1343, as said below
- edge_receiver: int32 [327680], P(('patch', 'band')), may hold values from 0 to 319
- block_counts: int32 [2560], P(('patch', 'band')), may hold values from 16 to 128, as said below
- send_rows: int32 [128, 128, 8], P(('patch', 'band')), may hold values from 0 to 319
- edge_first_weight: bfloat16 [2, 1536, 512], replicated, may hold values from -0.15625 to 0.15625
- edge_first_bias: float32 [2, 512], replicated, may hold values from -3 to 3
- edge_second_weight: bfloat16 [2, 512, 512], replicated
- edge_gain: float32 [2, 512], replicated, may hold values from 0.1 to 1.9
- edge_offset: float32 [2, 512], replicated, may hold values from -3 to 3
- node_first_weight: bfloat16 [2, 1024, 512], replicated, may hold values from -0.1875 to 0.1875
- node_first_bias: float32 [2, 512], replicated, may hold values from -3 to 3
- node_second_weight: bfloat16 [2, 512, 512], replicated
- node_gain: float32 [2, 512], replicated, may hold values from 0.1 to 1.9
- node_offset: float32 [2, 512], replicated, may hold values from -3 to 3
Outputs:
- new_nodes: float32 [40960, 512], P(('patch', 'band'))
- new_edges: float32 [327680, 512], P(('patch', 'band'))
Inputs may be any that keep to these rules, and one draw needn't show every extreme that they name: `edge_sender`: an entry below 320 names a node row of the edge's own device; an entry k above names slot (k - 320) % 8 of the rows that device (k - 320) // 8 sends to the edge's device. `block_counts`: the used slots of a block are its first ones; every device has a full block. send_rows[d, q] lists node rows of device d, numbered within d, that device q receives from d.
All inputs are finite; a program needn't handle non-finite values.
Results may differ from a plain program's by a relative error of at most 0.0045.
Values may be sent and summed in bfloat16 or wider, within the bound.
A program may use at most 128 MiB of HBM per device.

v0:
```python
import jax
import jax.numpy as jnp
from jax import lax
from jax.sharding import PartitionSpec as P

epsilon = 1e-05


def layer_norm(values, norm_gain, norm_offset):
    centre = values - jnp.mean(values, axis=-1, keepdims=True)
    spread = jnp.mean(centre * centre, axis=-1, keepdims=True)
    return centre * lax.rsqrt(spread + epsilon) * norm_gain + norm_offset


def perceptron(pieces, first_weight, first_bias, second_weight, norm_gain, norm_offset):
    columns = pieces[0].shape[1]
    running = first_bias
    for position in range(len(pieces)):
        running = running + jnp.dot(
            pieces[position],
            first_weight[position * columns : (position + 1) * columns],
            preferred_element_type=jnp.float32,
        )
    active = (running * jax.nn.sigmoid(running)).astype(jnp.bfloat16)
    result = jnp.dot(active, second_weight, preferred_element_type=jnp.float32)
    return layer_norm(result, norm_gain, norm_offset)


def fetch_halo(node_low, send_lists):
    outgoing = node_low[send_lists]
    return lax.all_to_all(outgoing, ("patch", "band"), split_axis=0, concat_axis=0, tiled=True)


def shards(
    latents,
    edge_latents,
    edge_sender,
    edge_receiver,
    block_counts,
    send_rows,
    edge_first_weight,
    edge_first_bias,
    edge_second_weight,
    edge_gain,
    edge_offset,
    node_first_weight,
    node_first_bias,
    node_second_weight,
    node_gain,
    node_offset,
):
    layers = edge_first_weight.shape[0]
    send_lists = send_rows[0]
    block_length = edge_sender.shape[0] // block_counts.shape[0]
    usable = (jnp.arange(block_length, dtype=jnp.int32)[None, :] < block_counts[:, None]).reshape(
        -1
    )
    first_rows = None
    node_state = lax.all_to_all(latents, "band", split_axis=0, concat_axis=1, tiled=True)
    edge_state = edge_latents
    node_count = node_state.shape[0]
    matches = jnp.arange(node_count, dtype=jnp.int32)[:, None] == edge_receiver[None, :]
    receiver_hot = matches.astype(jnp.bfloat16)
    summing_hot = (matches & usable[None, :]).astype(jnp.bfloat16)
    for layer_index in range(layers):
        node_low = node_state.astype(jnp.bfloat16)
        incoming = fetch_halo(node_low, send_lists)
        sender_table = jnp.concatenate([node_low, incoming.reshape(-1, node_low.shape[1])], axis=0)
        receiver_rows = lax.dot_general(
            receiver_hot, node_low, (((0,), (0,)), ((), ())), preferred_element_type=jnp.float32
        ).astype(jnp.bfloat16)
        edge_low = edge_state.astype(jnp.bfloat16)
        update = perceptron(
            (edge_low, sender_table[edge_sender], receiver_rows),
            edge_first_weight[layer_index],
            edge_first_bias[layer_index],
            edge_second_weight[layer_index],
            edge_gain[layer_index],
            edge_offset[layer_index],
        )
        edge_state = edge_state + jnp.where(usable[:, None], update, jnp.zeros_like(update))
        edge_out_low = edge_state.astype(jnp.bfloat16)
        summed = jnp.dot(summing_hot, edge_out_low, preferred_element_type=jnp.float32)
        summed_low = summed.astype(jnp.bfloat16)
        node_state = node_state + perceptron(
            (node_low, summed_low),
            node_first_weight[layer_index],
            node_first_bias[layer_index],
            node_second_weight[layer_index],
            node_gain[layer_index],
            node_offset[layer_index],
        )
    return (node_state, edge_state)


def solution(mesh):
    return jax.shard_map(
        shards,
        mesh=mesh,
        in_specs=(
            P("patch", "band"),
            P(("patch", "band"), None),
            P(("patch", "band")),
            P(("patch", "band")),
            P(("patch", "band")),
            P(("patch", "band"), None, None),
            P(),
            P(),
            P(),
            P(),
            P(),
            P(),
            P(),
            P(),
            P(),
            P(),
        ),
        out_specs=(P(("patch", "band"), None), P(("patch", "band"), None)),
        check_vma=False,
    )
```

profile of v0, /device:TPU:1, one launch (start us, length us, event | category | flops | bytes accessed | tf_op | source)
XLA Modules:
  0.0 172.8 jit_solution(914075629936271546)
XLA Ops:
  0.6 3.5 %all-to-all-start = ((f32[2,320,256]{2,1,0:T(8,128)}), f32[2,320,256]{2,1,0:T(8,128)S(1)}, u32[]{:S(2)}, u32[]{:S(2)}) async-start(f32[2,320,256]{2,1,0:T(8,128)} %bitcast.107), calls=%async_computation | async-start | bytes 1310720 | tf_op jit(solution)/shard_map/all_to_all | solution.py:59
  8.9 6.4 %fusion.6 = f32[2560,512]{1,0:T(8,128)} fusion(f32[2560,512]{1,0:T(8,128)} %param.17, bf16[2,1536,512]{2,1,0:T(8,128)(2,1)} %param.22), kind=kOutput, calls=%fused_computation.17 | convolution fusion | flops 1343488000 | bytes 11010048 | tf_op jit(solution)/shard_map/dot_general | solution.py:19
  15.6 5.1 %gather_fusion = bf16[1024,512]{1,0:T(8,128)(2,1)} fusion(bf16[320,512]{1,0:T(8,128)(2,1)S(1)} %convert_element_type.50, s32[1024]{0:T(1024)S(1)} %broadcast_clamp_fusion), kind=kCustom, calls=%fused_computation | custom fusion | bytes 2101248 | tf_op jit(solution)/shard_map/gather | solution.py:30
  20.7 12.5 %all-to-all-start.1 = ((bf16[128,8,512]{2,1,0:T(8,128)(2,1)}), bf16[128,8,512]{2,1,0:T(8,128)(2,1)}, u32[]{:S(2)}, u32[]{:S(2)}) async-start(bf16[128,8,512]{2,1,0:T(8,128)(2,1)} %bitcast.104), calls=%async_computation.1 | async-start | bytes 2097152 | tf_op jit(solution)/shard_map/all_to_all | solution.py:31
  33.2 5.9 %copy.32 = f32[2560,512]{0,1:T(8,128)} copy(f32[2560,512]{1,0:T(8,128)} %param.17) | data formatting | bytes 10485760 | tf_op args[1]
  39.2 2.2 %convolution_add_fusion.3 = f32[320,512]{1,0:T(8,128)} fusion(bf16[320,512]{1,0:T(8,128)(2,1)S(1)} %bitcast.106, bf16[2,1024,512]{2,1,0:T(8,128)(2,1)} %param.27, f32[512]{0:T(512)S(1)} %bitcast.115), kind=kOutput, calls=%fused_computation.35 | convolution fusion | flops 167936000 | bytes 1509376 | tf_op jit(solution)/shard_map/dot_general | solution.py:19
  41.4 3.0 %convolution_convert_fusion.1 = bf16[2560,512]{1,0:T(8,128)(2,1)} fusion(bf16[320,512]{1,0:T(8,128)(2,1)S(1)} %convert_element_type.50, s32[2560]{0:T(1024)S(1)} %copy-done.12), kind=kOutput, calls=%fused_computation.11 | convolution fusion | flops 840990720 | bytes 2959360 | tf_op jit(solution)/shard_map/dot_general | solution.py:69
  44.4 8.1 %all-to-all-done.1 = bf16[128,8,512]{2,1,0:T(8,128)(2,1)} async-done(((bf16[128,8,512]{2,1,0:T(8,128)(2,1)}), bf16[128,8,512]{2,1,0:T(8,128)(2,1)}, u32[]{:S(2)}, u32[]{:S(2)}) %all-to-all-start.1) | async-done | bytes 1048608 | tf_op jit(solution)/shard_map/all_to_all | solution.py:31
  52.6 1.3 pad_maximum_fusion
  53.9 8.2 %gather_fusion.1 = bf16[2560,512]{1,0:T(8,128)(2,1)} fusion(bf16[1344,512]{1,0:T(8,128)(2,1)S(1)} %pad_maximum_fusion, s32[3072]{0:T(1024)S(1)} %pad_clamp_fusion), kind=kCustom, calls=%fused_computation.1 | custom fusion | bytes 5253120 | tf_op jit(solution)/shard_map/gather | solution.py:74
  62.1 5.8 %fusion.61 = f32[2560,512]{1,0:T(8,128)} fusion(bf16[2560,512]{1,0:T(8,128)(2,1)} %gather_fusion.1, bf16[2,1536,512]{2,1,0:T(8,128)(2,1)} %param.22), kind=kOutput, calls=%fused_computation.59 | convolution fusion | flops 1342177280 | bytes 8388608 | tf_op jit(solution)/shard_map/dot_general | solution.py:19
  67.9 11.1 %fusion.92 = (f32[2560]{0:T(1024)S(1)}, f32[2560,512]{0,1:T(8,128)}) fusion(bf16[2,512,512]{2,1,0:T(8,128)(2,1)S(1)} %copy-done.10, f32[2560,512]{1,0:T(8,128)} %fusion.61, f32[2560,512]{1,0:T(8,128)} %fusion.6, bf16[2560,512]{1,0:T(8,128)(2,1)} %convolution_convert_fusion.1, f32[512]{0:T(512)S(1)} %bitcast.121, bf16[2,1536,512]{2,1,0:T(8,128)(2,1)} %param.22), kind=kOutput, calls=%fused_computation.101 | convolution fusion | flops 2696148480 | bytes 19410944 | tf_op jit(solution)/shard_map/dot_general | solution.py:25
  79.0 3.2 %multiply_reduce_fusion.1 = f32[2560]{0:T(1024)S(1)} fusion(f32[2560,512]{0,1:T(8,128)} %get-tuple-element.23, f32[2560]{0:T(1024)S(1)} %broadcast_multiply_fusion.1), kind=kLoop, calls=%fused_computation.8 | loop fusion | flops 3929600 | bytes 5263360 | tf_op jit(solution)/shard_map/reduce_sum | solution.py:11
  83.0 6.3 %select_add_fusion.1 = f32[2560,512]{0,1:T(8,128)} fusion(f32[2560,512]{0,1:T(8,128)} %copy.32, f32[2560,512]{0,1:T(8,128)S(1)} %copy-done.1, f32[512]{0:T(512)S(1)} %bitcast.119, f32[512]{0:T(512)S(1)} %bitcast.118, f32[2560]{0:T(1024)S(1)} %add_rsqrt_fusion.1, f32[2560]{0:T(1024)S(1)} %broadcast_multiply_fusion.1, pred[2560]{0:T(1024)(128)(4,1)S(1)} %fusion.82), kind=kLoop, calls=%fused_computation.7 | loop fusion | flops 7864320 | bytes 15755776 | tf_op jit(solution)/shard_map/add | solution.py:81
  89.3 4.1 %multiply_convert_fusion.3 = bf16[320,512]{1,0:T(8,128)(2,1)S(1)} fusion(f32[320,512]{1,0:T(8,128)S(1)} %copy-done.6, f32[2560,512]{0,1:T(8,128)} %select_add_fusion.1, s32[2560]{0:T(1024)S(1)} %copy-done.12, pred[2560]{0:T(1024)(128)(4,1)S(1)} %fusion.82, bf16[2,1024,512]{2,1,0:T(8,128)(2,1)} %param.27), kind=kOutput, calls=%fused_computation.44 | convolution fusion | flops 1010728960 | bytes 6763008 | tf_op jit(solution)/shard_map/dot_general | solution.py:19
  94.3 5.1 %gather_fusion.2 = bf16[1024,512]{1,0:T(8,128)(2,1)} fusion(bf16[320,512]{1,0:T(8,128)(2,1)S(1)} %fusion.85, s32[1024]{0:T(1024)S(1)} %broadcast_clamp_fusion), kind=kCustom, calls=%fused_computation.2 | custom fusion | bytes 2101248 | tf_op jit(solution)/shard_map/gather | solution.py:30
  99.4 4.1 %all-to-all-start.2 = ((bf16[128,8,512]{2,1,0:T(8,128)(2,1)}), bf16[128,8,512]{2,1,0:T(8,128)(2,1)S(1)}, u32[]{:S(2)}, u32[]{:S(2)}) async-start(bf16[128,8,512]{2,1,0:T(8,128)(2,1)} %bitcast.23), calls=%async_computation.2 | async-start | bytes 2097152 | tf_op jit(solution)/shard_map/all_to_all | solution.py:31
  103.5 2.4 %convolution_add_fusion.1 = f32[320,512]{1,0:T(8,128)} fusion(bf16[320,512]{1,0:T(8,128)(2,1)S(1)} %fusion.85, bf16[2,1024,512]{2,1,0:T(8,128)(2,1)} %param.27, f32[512]{0:T(512)S(1)} %bitcast.114), kind=kOutput, calls=%fused_computation.33 | convolution fusion | flops 167936000 | bytes 1509376 | tf_op jit(solution)/shard_map/dot_general | solution.py:19
  105.9 3.0 %convolution_convert_fusion = bf16[2560,512]{1,0:T(8,128)(2,1)} fusion(bf16[320,512]{1,0:T(8,128)(2,1)S(1)} %fusion.85, s32[2560]{0:T(1024)S(1)} %copy-done.12), kind=kOutput, calls=%fused_computation.10 | convolution fusion | flops 840990720 | bytes 2959360 | tf_op jit(solution)/shard_map/dot_general | solution.py:69
  108.9 4.9 %fusion.16 = f32[2560,512]{1,0:T(8,128)} fusion(f32[2560,512]{0,1:T(8,128)S(1)} %bitcast.99, bf16[2,1536,512]{2,1,0:T(8,128)(2,1)} %param.22), kind=kOutput, calls=%fused_computation.29 | convolution fusion | flops 1343488000 | bytes 11010048 | tf_op jit(solution)/shard_map/dot_general | solution.py:19
  113.9 9.5 %all-to-all-done.2 = bf16[128,8,512]{2,1,0:T(8,128)(2,1)S(1)} async-done(((bf16[128,8,512]{2,1,0:T(8,128)(2,1)}), bf16[128,8,512]{2,1,0:T(8,128)(2,1)S(1)}, u32[]{:S(2)}, u32[]{:S(2)}) %all-to-all-start.2) | async-done | bytes 1048608 | tf_op jit(solution)/shard_map/all_to_all | solution.py:31
  123.4 1.0 copy-done.2
  124.4 1.3 pad_maximum_fusion.1
  125.7 8.2 %gather_fusion.3 = bf16[2560,512]{1,0:T(8,128)(2,1)} fusion(bf16[1344,512]{1,0:T(8,128)(2,1)S(1)} %pad_maximum_fusion.1, s32[3072]{0:T(1024)S(1)} %pad_clamp_fusion), kind=kCustom, calls=%fused_computation.3 | custom fusion | bytes 5253120 | tf_op jit(solution)/shard_map/gather | solution.py:74
  133.9 5.8 %fusion.51 = f32[2560,512]{1,0:T(8,128)} fusion(bf16[2560,512]{1,0:T(8,128)(2,1)} %gather_fusion.3, bf16[2,1536,512]{2,1,0:T(8,128)(2,1)} %param.22), kind=kOutput, calls=%fused_computation.50 | convolution fusion | flops 1342177280 | bytes 8388608 | tf_op jit(solution)/shard_map/dot_general | solution.py:19
  139.7 11.1 %fusion.96 = (f32[2560]{0:T(1024)S(1)}, f32[2560,512]{0,1:T(8,128)}) fusion(bf16[2,512,512]{2,1,0:T(8,128)(2,1)S(1)} %copy-done.11, f32[2560,512]{1,0:T(8,128)} %fusion.51, f32[2560,512]{1,0:T(8,128)} %fusion.16, bf16[2560,512]{1,0:T(8,128)(2,1)} %convolution_convert_fusion, f32[512]{0:T(512)S(1)} %bitcast.120, bf16[2,1536,512]{2,1,0:T(8,128)(2,1)} %param.22), kind=kOutput, calls=%fused_computation.103 | convolution fusion | flops 2696148480 | bytes 19410944 | tf_op jit(solution)/shard_map/dot_general | solution.py:25
  150.8 3.2 %multiply_reduce_fusion = f32[2560]{0:T(1024)S(1)} fusion(f32[2560,512]{0,1:T(8,128)} %get-tuple-element.27, f32[2560]{0:T(1024)S(1)} %broadcast_multiply_fusion), kind=kLoop, calls=%fused_computation.5 | loop fusion | flops 3929600 | bytes 5263360 | tf_op jit(solution)/shard_map/reduce_sum | solution.py:11
  154.0 0.8 copy-done
  154.8 6.2 %select_add_fusion = f32[2560,512]{0,1:T(8,128)} fusion(f32[2560,512]{0,1:T(8,128)} %select_add_fusion.1, f32[2560,512]{0,1:T(8,128)S(1)} %copy-done, f32[512]{0:T(512)S(1)} %bitcast.117, f32[512]{0:T(512)S(1)} %bitcast.116, f32[2560]{0:T(1024)S(1)} %add_rsqrt_fusion, f32[2560]{0:T(1024)S(1)} %broadcast_multiply_fusion, pred[2560]{0:T(1024)(128)(4,1)S(1)} %fusion.82), kind=kLoop, calls=%fused_computation.4 | loop fusion | flops 7864320 | bytes 15755776 | tf_op jit(solution)/shard_map/add | solution.py:81
  161.0 5.9 %copy.33 = f32[2560,512]{1,0:T(8,128)} copy(f32[2560,512]{0,1:T(8,128)} %select_add_fusion) | data formatting | bytes 10485760
  166.9 4.1 %multiply_convert_fusion.2 = bf16[320,512]{1,0:T(8,128)(2,1)S(1)} fusion(f32[320,512]{1,0:T(8,128)S(1)} %copy-done.5, f32[2560,512]{0,1:T(8,128)} %select_add_fusion, s32[2560]{0:T(1024)S(1)} %copy-done.12, pred[2560]{0:T(1024)(128)(4,1)S(1)} %fusion.82, bf16[2,1024,512]{2,1,0:T(8,128)(2,1)} %param.27), kind=kOutput, calls=%fused_computation.41 | convolution fusion | flops 1010728960 | bytes 6763008 | tf_op jit(solution)/shard_map/dot_general | solution.py:19
  171.7 1.1 add_add_fusion
  (60 shorter events, 7.5 us)
Async XLA Ops:
  0.6 14.8 %all-to-all-start = ((f32[2,320,256]{2,1,0:T(8,128)}), f32[2,320,256]{2,1,0:T(8,128)S(1)}, u32[]{:S(2)}, u32[]{:S(2)}) async-start(f32[2,320,256]{2,1,0:T(8,128)} %bitcast.107), calls=%async_computation | async-start | bytes 1310720 | tf_op jit(solution)/shard_map/all_to_all | solution.py:59
  8.9 6.4 %copy-start.9 = (s32[20]{0:T(128)S(1)}, s32[20]{0:T(128)}, u32[]{:S(2)}) copy-start(s32[20]{0:T(128)} %param.20) | copy-start | bytes 244
  8.9 6.5 %copy-start.7 = (s32[2560]{0:T(1024)S(1)}, s32[2560]{0:T(1024)}, u32[]{:S(2)}) copy-start(s32[2560]{0:T(1024)} %param.18) | copy-start | bytes 30724
  20.7 31.9 %all-to-all-start.1 = ((bf16[128,8,512]{2,1,0:T(8,128)(2,1)}), bf16[128,8,512]{2,1,0:T(8,128)(2,1)}, u32[]{:S(2)}, u32[]{:S(2)}) async-start(bf16[128,8,512]{2,1,0:T(8,128)(2,1)} %bitcast.104), calls=%async_computation.1 | async-start | bytes 2097152 | tf_op jit(solution)/shard_map/all_to_all | solution.py:31
  33.2 5.9 %copy-start.8 = (f32[2,512]{1,0:T(2,128)S(1)}, f32[2,512]{1,0:T(2,128)}, u32[]{:S(2)}) copy-start(f32[2,512]{1,0:T(2,128)} %param.31) | copy-start | bytes 12292
  33.2 8.2 %copy-start.12 = (s32[2560]{0:T(1024)S(1)}, s32[2560]{0:T(1024)}, u32[]{:S(2)}) copy-start(s32[2560]{0:T(1024)} %param.19) | copy-start | bytes 30724
  62.1 5.8 %copy-start.10 = (bf16[2,512,512]{2,1,0:T(8,128)(2,1)S(1)}, bf16[2,512,512]{2,1,0:T(8,128)(2,1)}, u32[]{:S(2)}) copy-start(bf16[2,512,512]{2,1,0:T(8,128)(2,1)} %param.24) | copy-start | bytes 3145732
  78.9 4.0 %copy-start.1 = (f32[2560,512]{0,1:T(8,128)S(1)}, f32[2560,512]{0,1:T(8,128)}, u32[]{:S(2)}) copy-start(f32[2560,512]{0,1:T(8,128)} %get-tuple-element.23) | copy-start | bytes 15728644
  83.0 6.3 %copy-start.6 = (f32[320,512]{1,0:T(8,128)S(1)}, f32[320,512]{1,0:T(8,128)}, u32[]{:S(2)}) copy-start(f32[320,512]{1,0:T(8,128)} %convolution_add_fusion.3) | copy-start | bytes 1966084
  89.3 4.1 %copy-start.3 = (bf16[2,512,512]{2,1,0:T(8,128)(2,1)S(1)}, bf16[2,512,512]{2,1,0:T(8,128)(2,1)}, u32[]{:S(2)}) copy-start(bf16[2,512,512]{2,1,0:T(8,128)(2,1)} %param.29) | copy-start | bytes 3145732
  99.4 24.0 %all-to-all-start.2 = ((bf16[128,8,512]{2,1,0:T(8,128)(2,1)}), bf16[128,8,512]{2,1,0:T(8,128)(2,1)S(1)}, u32[]{:S(2)}, u32[]{:S(2)}) async-start(bf16[128,8,512]{2,1,0:T(8,128)(2,1)} %bitcast.23), calls=%async_computation.2 | async-start | bytes 2097152 | tf_op jit(solution)/shard_map/all_to_all | solution.py:31
  103.5 5.4 %slice-start = ((s8[5242880]{0:T(1024)(128)(4,1)}), s8[4194304]{0:T(1024)(128)(4,1)S(1)}, s32[]{:S(2)}) async-start(s8[5242880]{0:T(1024)(128)(4,1)} %bitcast.98), calls=%async_computation.3 | async-start | bytes 8388608
  105.9 3.1 %slice-start.1 = ((s8[5242880]{0:T(1024)(128)(4,1)}), s8[1048576]{0:T(1024)(128)(4,1)S(1)}, s32[]{:S(2)}) async-start(s8[5242880]{0:T(1024)(128)(4,1)} %bitcast.98), calls=%async_computation.4 | async-start | bytes 2097152
  123.4 1.0 copy-start.2
  133.9 5.8 %copy-start.11 = (bf16[2,512,512]{2,1,0:T(8,128)(2,1)S(1)}, bf16[2,512,512]{2,1,0:T(8,128)(2,1)}, u32[]{:S(2)}) copy-start(bf16[2,512,512]{2,1,0:T(8,128)(2,1)} %param.24) | copy-start | bytes 3145732
  150.8 4.0 %copy-start = (f32[2560,512]{0,1:T(8,128)S(1)}, f32[2560,512]{0,1:T(8,128)}, u32[]{:S(2)}) copy-start(f32[2560,512]{0,1:T(8,128)} %get-tuple-element.27) | copy-start | bytes 15728644
  161.0 5.9 %copy-start.5 = (f32[320,512]{1,0:T(8,128)S(1)}, f32[320,512]{1,0:T(8,128)}, u32[]{:S(2)}) copy-start(f32[320,512]{1,0:T(8,128)} %convolution_add_fusion.1) | copy-start | bytes 1966084
  166.9 4.1 %copy-start.4 = (bf16[2,512,512]{2,1,0:T(8,128)(2,1)S(1)}, bf16[2,512,512]{2,1,0:T(8,128)(2,1)}, u32[]{:S(2)}) copy-start(bf16[2,512,512]{2,1,0:T(8,128)(2,1)} %param.29) | copy-start | bytes 3145732
where the time goes:
time: 174 us; the launch traced here: 173 us
  matrix products  64.8 us (37%)
  local copies, waits for them, and re-layouts  45.2 us (26%)
  other arithmetic  24.3 us (14%)
  starting transfers between devices  20.1 us (12%)
  waiting for transfers between devices  17.6 us (10%)
    dot_general x8, matrix products, perceptron(): jnp.dot(pieces[position], first_weight[position * columns:(position + 1)...  35.6 us
    dot_general x4, matrix products, perceptron(): result = jnp.dot(active, second_weight, preferred_element_type=jnp.float32)  23 us
    all_to_all x2, waiting for transfers between devices, fetch_halo(): lax.all_to_all(outgoing, ('patch', 'band'), split_axis=0, concat_axis=0,...  17.6 us
    all_to_all x2, starting transfers between devices, fetch_halo(): lax.all_to_all(outgoing, ('patch', 'band'), split_axis=0, concat_axis=0,...  16.6 us
    gather x2, local copies, waits for them, and re-layouts, shards(): sender_table[edge_sender]  16.4 us
    unnamed x32, local copies, waits for them, and re-layouts  14.5 us
    add x2, other arithmetic, shards(): edge_state + jnp.where(usable[:, None], update, jnp.zeros_like(update))  12.5 us
    gather x2, local copies, waits for them, and re-layouts, fetch_halo(): outgoing = node_low[send_lists]  10.2 us
  transfers between devices with their start and end apart: 3, of which 2 were waited for; matrix products, arithmetic and copies ran while one was open for 19% of the time, Pallas kernels for 0%

commit v1 on v0

--- a/solution.py
+++ b/solution.py
@@ -56,7 +56,10 @@
         -1
     )
     first_rows = None
-    node_state = lax.all_to_all(latents, "band", split_axis=0, concat_axis=1, tiled=True)
+    node_state = jnp.concatenate(
+        lax.all_to_all(jnp.stack(jnp.split(latents, lax.axis_size("band"), axis=0)), "band", 0, 0),
+        axis=1,
+    )
     edge_state = edge_latents
     node_count = node_state.shape[0]
     matches = jnp.arange(node_count, dtype=jnp.int32)[:, None] == edge_receiver[None, :]

time: 174 us -> 176 us (1.011)
  no operation moved by 1% of the time
where the time goes in v1:
time: 176 us; the launch traced here: 175 us
  matrix products  64.8 us (37%)
  local copies, waits for them, and re-layouts  46.4 us (26%)
  other arithmetic  25.2 us (14%)
  starting transfers between devices  20.1 us (11%)
  waiting for transfers between devices  17.6 us (10%)
    dot_general x8, matrix products, perceptron(): jnp.dot(pieces[position], first_weight[position * columns:(position + 1)...  35.6 us
    dot_general x4, matrix products, perceptron(): result = jnp.dot(active, second_weight, preferred_element_type=jnp.float32)  23.1 us
    all_to_all x2, waiting for transfers between devices, fetch_halo(): lax.all_to_all(outgoing, ('patch', 'band'), split_axis=0, concat_axis=0,...  17.6 us
    all_to_all x2, starting transfers between devices, fetch_halo(): lax.all_to_all(outgoing, ('patch', 'band'), split_axis=0, concat_axis=0,...  16.6 us
    gather x2, local copies, waits for them, and re-layouts, shards(): sender_table[edge_sender]  16.4 us
    unnamed x32, local copies, waits for them, and re-layouts  14.5 us
    add x2, other arithmetic, shards(): edge_state + jnp.where(usable[:, None], update, jnp.zeros_like(update))  12.5 us
    gather x2, local copies, waits for them, and re-layouts, fetch_halo(): outgoing = node_low[send_lists]  10.2 us
  transfers between devices with their start and end apart: 3, of which 2 were waited for; matrix products, arithmetic and copies ran while one was open for 19% of the time, Pallas kernels for 0%

profile of v1, /device:TPU:1, one launch (start us, length us, event | category | flops | bytes accessed | tf_op | source)
XLA Modules:
  0.0 174.9 jit_solution(10796314809711544578)
XLA Ops:
  0.6 1.1 slice_bitcast_fusion.1
  2.6 3.5 %all-to-all-start = ((f32[2,320,256]{2,1,0:T(8,128)}), f32[2,320,256]{2,1,0:T(8,128)S(1)}, u32[]{:S(2)}, u32[]{:S(2)}) async-start(f32[2,320,256]{2,1,0:T(8,128)} %pad_maximum_fusion.2), calls=%async_computation | async-start | bytes 1310720 | tf_op jit(solution)/shard_map/all_to_all | solution.py:60
  10.9 6.4 %fusion.6 = f32[2560,512]{1,0:T(8,128)} fusion(f32[2560,512]{1,0:T(8,128)} %param.17, bf16[2,1536,512]{2,1,0:T(8,128)(2,1)} %param.22), kind=kOutput, calls=%fused_computation.17 | convolution fusion | flops 1343488000 | bytes 11010048 | tf_op jit(solution)/shard_map/dot_general | solution.py:19
  17.6 5.1 %gather_fusion = bf16[1024,512]{1,0:T(8,128)(2,1)} fusion(bf16[320,512]{1,0:T(8,128)(2,1)S(1)} %convert_element_type.50, s32[1024]{0:T(1024)S(1)} %broadcast_clamp_fusion), kind=kCustom, calls=%fused_computation | custom fusion | bytes 2101248 | tf_op jit(solution)/shard_map/gather | solution.py:30
  22.6 12.5 %all-to-all-start.1 = ((bf16[128,8,512]{2,1,0:T(8,128)(2,1)}), bf16[128,8,512]{2,1,0:T(8,128)(2,1)}, u32[]{:S(2)}, u32[]{:S(2)}) async-start(bf16[128,8,512]{2,1,0:T(8,128)(2,1)} %bitcast.107), calls=%async_computation.1 | async-start | bytes 2097152 | tf_op jit(solution)/shard_map/all_to_all | solution.py:31
  35.2 5.9 %copy.24 = f32[2560,512]{0,1:T(8,128)} copy(f32[2560,512]{1,0:T(8,128)} %param.17) | data formatting | bytes 10485760 | tf_op args[1]
  41.2 2.2 %convolution_add_fusion.3 = f32[320,512]{1,0:T(8,128)} fusion(bf16[320,512]{1,0:T(8,128)(2,1)S(1)} %bitcast.109, bf16[2,1024,512]{2,1,0:T(8,128)(2,1)} %param.27, f32[512]{0:T(512)S(1)} %bitcast.117), kind=kOutput, calls=%fused_computation.35 | convolution fusion | flops 167936000 | bytes 1509376 | tf_op jit(solution)/shard_map/dot_general | solution.py:19
  43.4 3.0 %convolution_convert_fusion.1 = bf16[2560,512]{1,0:T(8,128)(2,1)} fusion(bf16[320,512]{1,0:T(8,128)(2,1)S(1)} %convert_element_type.50, s32[2560]{0:T(1024)S(1)} %copy-done.12), kind=kOutput, calls=%fused_computation.11 | convolution fusion | flops 840990720 | bytes 2959360 | tf_op jit(solution)/shard_map/dot_general | solution.py:72
  46.4 8.1 %all-to-all-done.1 = bf16[128,8,512]{2,1,0:T(8,128)(2,1)} async-done(((bf16[128,8,512]{2,1,0:T(8,128)(2,1)}), bf16[128,8,512]{2,1,0:T(8,128)(2,1)}, u32[]{:S(2)}, u32[]{:S(2)}) %all-to-all-start.1) | async-done | bytes 1048608 | tf_op jit(solution)/shard_map/all_to_all | solution.py:31
  54.5 1.3 pad_maximum_fusion
  55.9 8.2 %gather_fusion.1 = bf16[2560,512]{1,0:T(8,128)(2,1)} fusion(bf16[1344,512]{1,0:T(8,128)(2,1)S(1)} %pad_maximum_fusion, s32[3072]{0:T(1024)S(1)} %pad_clamp_fusion), kind=kCustom, calls=%fused_computation.1 | custom fusion | bytes 5253120 | tf_op jit(solution)/shard_map/gather | solution.py:77
  64.1 5.8 %fusion.61 = f32[2560,512]{1,0:T(8,128)} fusion(bf16[2560,512]{1,0:T(8,128)(2,1)} %gather_fusion.1, bf16[2,1536,512]{2,1,0:T(8,128)(2,1)} %param.22), kind=kOutput, calls=%fused_computation.60 | convolution fusion | flops 1342177280 | bytes 8388608 | tf_op jit(solution)/shard_map/dot_general | solution.py:19
  69.8 11.1 %fusion.92 = (f32[2560]{0:T(1024)S(1)}, f32[2560,512]{0,1:T(8,128)}) fusion(bf16[2,512,512]{2,1,0:T(8,128)(2,1)S(1)} %copy-done.10, f32[2560,512]{1,0:T(8,128)} %fusion.61, f32[2560,512]{1,0:T(8,128)} %fusion.6, bf16[2560,512]{1,0:T(8,128)(2,1)} %convolution_convert_fusion.1, f32[512]{0:T(512)S(1)} %bitcast.123, bf16[2,1536,512]{2,1,0:T(8,128)(2,1)} %param.22), kind=kOutput, calls=%fused_computation.104 | convolution fusion | flops 2696148480 | bytes 19410944 | tf_op jit(solution)/shard_map/dot_general | solution.py:25
  81.0 3.2 %multiply_reduce_fusion.1 = f32[2560]{0:T(1024)S(1)} fusion(f32[2560,512]{0,1:T(8,128)} %get-tuple-element.21, f32[2560]{0:T(1024)S(1)} %broadcast_multiply_fusion.1), kind=kLoop, calls=%fused_computation.8 | loop fusion | flops 3929600 | bytes 5263360 | tf_op jit(solution)/shard_map/reduce_sum | solution.py:11
  85.0 6.3 %select_add_fusion.1 = f32[2560,512]{0,1:T(8,128)} fusion(f32[2560,512]{0,1:T(8,128)} %copy.24, f32[2560,512]{0,1:T(8,128)S(1)} %copy-done.1, f32[512]{0:T(512)S(1)} %bitcast.121, f32[512]{0:T(512)S(1)} %bitcast.120, f32[2560]{0:T(1024)S(1)} %add_rsqrt_fusion.1, f32[2560]{0:T(1024)S(1)} %broadcast_multiply_fusion.1, pred[2560]{0:T(1024)(128)(4,1)S(1)} %fusion.82), kind=kLoop, calls=%fused_computation.7 | loop fusion | flops 7864320 | bytes 15755776 | tf_op jit(solution)/shard_map/add | solution.py:84
  91.3 4.1 %multiply_convert_fusion.3 = bf16[320,512]{1,0:T(8,128)(2,1)S(1)} fusion(f32[320,512]{1,0:T(8,128)S(1)} %copy-done.6, f32[2560,512]{0,1:T(8,128)} %select_add_fusion.1, s32[2560]{0:T(1024)S(1)} %copy-done.12, pred[2560]{0:T(1024)(128)(4,1)S(1)} %fusion.82, bf16[2,1024,512]{2,1,0:T(8,128)(2,1)} %param.27), kind=kOutput, calls=%fused_computation.45 | convolution fusion | flops 1010728960 | bytes 6763008 | tf_op jit(solution)/shard_map/dot_general | solution.py:19
  96.3 5.1 %gather_fusion.2 = bf16[1024,512]{1,0:T(8,128)(2,1)} fusion(bf16[320,512]{1,0:T(8,128)(2,1)S(1)} %fusion.85, s32[1024]{0:T(1024)S(1)} %broadcast_clamp_fusion), kind=kCustom, calls=%fused_computation.2 | custom fusion | bytes 2101248 | tf_op jit(solution)/shard_map/gather | solution.py:30
  101.4 4.1 %all-to-all-start.2 = ((bf16[128,8,512]{2,1,0:T(8,128)(2,1)}), bf16[128,8,512]{2,1,0:T(8,128)(2,1)S(1)}, u32[]{:S(2)}, u32[]{:S(2)}) async-start(bf16[128,8,512]{2,1,0:T(8,128)(2,1)} %bitcast.24), calls=%async_computation.2 | async-start | bytes 2097152 | tf_op jit(solution)/shard_map/all_to_all | solution.py:31
  105.5 2.4 %convolution_add_fusion.1 = f32[320,512]{1,0:T(8,128)} fusion(bf16[320,512]{1,0:T(8,128)(2,1)S(1)} %fusion.85, bf16[2,1024,512]{2,1,0:T(8,128)(2,1)} %param.27, f32[512]{0:T(512)S(1)} %bitcast.116), kind=kOutput, calls=%fused_computation.33 | convolution fusion | flops 167936000 | bytes 1509376 | tf_op jit(solution)/shard_map/dot_general | solution.py:19
  107.9 3.0 %convolution_convert_fusion = bf16[2560,512]{1,0:T(8,128)(2,1)} fusion(bf16[320,512]{1,0:T(8,128)(2,1)S(1)} %fusion.85, s32[2560]{0:T(1024)S(1)} %copy-done.12), kind=kOutput, calls=%fused_computation.10 | convolution fusion | flops 840990720 | bytes 2959360 | tf_op jit(solution)/shard_map/dot_general | solution.py:72
  110.9 4.9 %fusion.16 = f32[2560,512]{1,0:T(8,128)} fusion(f32[2560,512]{0,1:T(8,128)S(1)} %bitcast.102, bf16[2,1536,512]{2,1,0:T(8,128)(2,1)} %param.22), kind=kOutput, calls=%fused_computation.29 | convolution fusion | flops 1343488000 | bytes 11010048 | tf_op jit(solution)/shard_map/dot_general | solution.py:19
  115.9 9.5 %all-to-all-done.2 = bf16[128,8,512]{2,1,0:T(8,128)(2,1)S(1)} async-done(((bf16[128,8,512]{2,1,0:T(8,128)(2,1)}), bf16[128,8,512]{2,1,0:T(8,128)(2,1)S(1)}, u32[]{:S(2)}, u32[]{:S(2)}) %all-to-all-start.2) | async-done | bytes 1048608 | tf_op jit(solution)/shard_map/all_to_all | solution.py:31
  125.4 1.0 copy-done.2
  126.4 1.3 pad_maximum_fusion.1
  127.7 8.2 %gather_fusion.3 = bf16[2560,512]{1,0:T(8,128)(2,1)} fusion(bf16[1344,512]{1,0:T(8,128)(2,1)S(1)} %pad_maximum_fusion.1, s32[3072]{0:T(1024)S(1)} %pad_clamp_fusion), kind=kCustom, calls=%fused_computation.3 | custom fusion | bytes 5253120 | tf_op jit(solution)/shard_map/gather | solution.py:77
  135.9 5.8 %fusion.51 = f32[2560,512]{1,0:T(8,128)} fusion(bf16[2560,512]{1,0:T(8,128)(2,1)} %gather_fusion.3, bf16[2,1536,512]{2,1,0:T(8,128)(2,1)} %param.22), kind=kOutput, calls=%fused_computation.51 | convolution fusion | flops 1342177280 | bytes 8388608 | tf_op jit(solution)/shard_map/dot_general | solution.py:19
  141.7 11.1 %fusion.96 = (f32[2560]{0:T(1024)S(1)}, f32[2560,512]{0,1:T(8,128)}) fusion(bf16[2,512,512]{2,1,0:T(8,128)(2,1)S(1)} %copy-done.11, f32[2560,512]{1,0:T(8,128)} %fusion.51, f32[2560,512]{1,0:T(8,128)} %fusion.16, bf16[2560,512]{1,0:T(8,128)(2,1)} %convolution_convert_fusion, f32[512]{0:T(512)S(1)} %bitcast.122, bf16[2,1536,512]{2,1,0:T(8,128)(2,1)} %param.22), kind=kOutput, calls=%fused_computation.106 | convolution fusion | flops 2696148480 | bytes 19410944 | tf_op jit(solution)/shard_map/dot_general | solution.py:25
  152.8 3.2 %multiply_reduce_fusion = f32[2560]{0:T(1024)S(1)} fusion(f32[2560,512]{0,1:T(8,128)} %get-tuple-element.25, f32[2560]{0:T(1024)S(1)} %broadcast_multiply_fusion), kind=kLoop, calls=%fused_computation.5 | loop fusion | flops 3929600 | bytes 5263360 | tf_op jit(solution)/shard_map/reduce_sum | solution.py:11
  156.8 6.2 %select_add_fusion = f32[2560,512]{0,1:T(8,128)} fusion(f32[2560,512]{0,1:T(8,128)} %select_add_fusion.1, f32[2560,512]{0,1:T(8,128)S(1)} %copy-done, f32[512]{0:T(512)S(1)} %bitcast.119, f32[512]{0:T(512)S(1)} %bitcast.118, f32[2560]{0:T(1024)S(1)} %add_rsqrt_fusion, f32[2560]{0:T(1024)S(1)} %broadcast_multiply_fusion, pred[2560]{0:T(1024)(128)(4,1)S(1)} %fusion.82), kind=kLoop, calls=%fused_computation.4 | loop fusion | flops 7864320 | bytes 15755776 | tf_op jit(solution)/shard_map/add | solution.py:84
  163.0 5.9 %copy.25 = f32[2560,512]{1,0:T(8,128)} copy(f32[2560,512]{0,1:T(8,128)} %select_add_fusion) | data formatting | bytes 10485760
  169.0 4.1 %multiply_convert_fusion.2 = bf16[320,512]{1,0:T(8,128)(2,1)S(1)} fusion(f32[320,512]{1,0:T(8,128)S(1)} %copy-done.5, f32[2560,512]{0,1:T(8,128)} %select_add_fusion, s32[2560]{0:T(1024)S(1)} %copy-done.12, pred[2560]{0:T(1024)(128)(4,1)S(1)} %fusion.82, bf16[2,1024,512]{2,1,0:T(8,128)(2,1)} %param.27), kind=kOutput, calls=%fused_computation.42 | convolution fusion | flops 1010728960 | bytes 6763008 | tf_op jit(solution)/shard_map/dot_general | solution.py:19
  173.8 1.1 add_add_fusion
  (62 shorter events, 9.1 us)
Async XLA Ops:
  2.6 14.8 %all-to-all-start = ((f32[2,320,256]{2,1,0:T(8,128)}), f32[2,320,256]{2,1,0:T(8,128)S(1)}, u32[]{:S(2)}, u32[]{:S(2)}) async-start(f32[2,320,256]{2,1,0:T(8,128)} %pad_maximum_fusion.2), calls=%async_computation | async-start | bytes 1310720 | tf_op jit(solution)/shard_map/all_to_all | solution.py:60
  10.9 6.4 %copy-start.9 = (s32[20]{0:T(128)S(1)}, s32[20]{0:T(128)}, u32[]{:S(2)}) copy-start(s32[20]{0:T(128)} %param.20) | copy-start | bytes 244
  10.9 6.5 %copy-start.7 = (s32[2560]{0:T(1024)S(1)}, s32[2560]{0:T(1024)}, u32[]{:S(2)}) copy-start(s32[2560]{0:T(1024)} %param.18) | copy-start | bytes 30724
  22.6 31.9 %all-to-all-start.1 = ((bf16[128,8,512]{2,1,0:T(8,128)(2,1)}), bf16[128,8,512]{2,1,0:T(8,128)(2,1)}, u32[]{:S(2)}, u32[]{:S(2)}) async-start(bf16[128,8,512]{2,1,0:T(8,128)(2,1)} %bitcast.107), calls=%async_computation.1 | async-start | bytes 2097152 | tf_op jit(solution)/shard_map/all_to_all | solution.py:31
  35.2 5.9 %copy-start.8 = (f32[2,512]{1,0:T(2,128)S(1)}, f32[2,512]{1,0:T(2,128)}, u32[]{:S(2)}) copy-start(f32[2,512]{1,0:T(2,128)} %param.31) | copy-start | bytes 12292
  35.2 8.2 %copy-start.12 = (s32[2560]{0:T(1024)S(1)}, s32[2560]{0:T(1024)}, u32[]{:S(2)}) copy-start(s32[2560]{0:T(1024)} %param.19) | copy-start | bytes 30724
  64.1 5.8 %copy-start.10 = (bf16[2,512,512]{2,1,0:T(8,128)(2,1)S(1)}, bf16[2,512,512]{2,1,0:T(8,128)(2,1)}, u32[]{:S(2)}) copy-start(bf16[2,512,512]{2,1,0:T(8,128)(2,1)} %param.24) | copy-start | bytes 3145732
  81.0 4.0 %copy-start.1 = (f32[2560,512]{0,1:T(8,128)S(1)}, f32[2560,512]{0,1:T(8,128)}, u32[]{:S(2)}) copy-start(f32[2560,512]{0,1:T(8,128)} %get-tuple-element.21) | copy-start | bytes 15728644
  85.0 6.3 %copy-start.6 = (f32[320,512]{1,0:T(8,128)S(1)}, f32[320,512]{1,0:T(8,128)}, u32[]{:S(2)}) copy-start(f32[320,512]{1,0:T(8,128)} %convolution_add_fusion.3) | copy-start | bytes 1966084
  91.3 4.1 %copy-start.3 = (bf16[2,512,512]{2,1,0:T(8,128)(2,1)S(1)}, bf16[2,512,512]{2,1,0:T(8,128)(2,1)}, u32[]{:S(2)}) copy-start(bf16[2,512,512]{2,1,0:T(8,128)(2,1)} %param.29) | copy-start | bytes 3145732
  101.4 24.0 %all-to-all-start.2 = ((bf16[128,8,512]{2,1,0:T(8,128)(2,1)}), bf16[128,8,512]{2,1,0:T(8,128)(2,1)S(1)}, u32[]{:S(2)}, u32[]{:S(2)}) async-start(bf16[128,8,512]{2,1,0:T(8,128)(2,1)} %bitcast.24), calls=%async_computation.2 | async-start | bytes 2097152 | tf_op jit(solution)/shard_map/all_to_all | solution.py:31
  105.5 5.4 %slice-start = ((s8[5242880]{0:T(1024)(128)(4,1)}), s8[4194304]{0:T(1024)(128)(4,1)S(1)}, s32[]{:S(2)}) async-start(s8[5242880]{0:T(1024)(128)(4,1)} %bitcast.101), calls=%async_computation.3 | async-start | bytes 8388608
  107.9 3.1 %slice-start.1 = ((s8[5242880]{0:T(1024)(128)(4,1)}), s8[1048576]{0:T(1024)(128)(4,1)S(1)}, s32[]{:S(2)}) async-start(s8[5242880]{0:T(1024)(128)(4,1)} %bitcast.101), calls=%async_computation.4 | async-start | bytes 2097152
  125.4 1.0 copy-start.2
  135.9 5.8 %copy-start.11 = (bf16[2,512,512]{2,1,0:T(8,128)(2,1)S(1)}, bf16[2,512,512]{2,1,0:T(8,128)(2,1)}, u32[]{:S(2)}) copy-start(bf16[2,512,512]{2,1,0:T(8,128)(2,1)} %param.24) | copy-start | bytes 3145732
  152.8 4.0 %copy-start = (f32[2560,512]{0,1:T(8,128)S(1)}, f32[2560,512]{0,1:T(8,128)}, u32[]{:S(2)}) copy-start(f32[2560,512]{0,1:T(8,128)} %get-tuple-element.25) | copy-start | bytes 15728644
  163.0 5.9 %copy-start.5 = (f32[320,512]{1,0:T(8,128)S(1)}, f32[320,512]{1,0:T(8,128)}, u32[]{:S(2)}) copy-start(f32[320,512]{1,0:T(8,128)} %convolution_add_fusion.1) | copy-start | bytes 1966084
  169.0 4.1 %copy-start.4 = (bf16[2,512,512]{2,1,0:T(8,128)(2,1)S(1)}, bf16[2,512,512]{2,1,0:T(8,128)(2,1)}, u32[]{:S(2)}) copy-start(bf16[2,512,512]{2,1,0:T(8,128)(2,1)} %param.29) | copy-start | bytes 3145732
